TPU v7x, 32 devices: a whole 2x2x4 slice. The times are simulated.
32 devices in a mesh: fsdp: 8 (over z, y), tp: 4 (over x, core).
Axes of the slice: x: 2, y: 2, z: 4, core: 2. Of those that a mesh axis runs over, the one named last changes fastest.
Arguments:
- hidden_in: bfloat16 [1024, 8192], P('fsdp'), may hold values from -6 to 6
- key_grad: bfloat16 [1024, 1024], P('fsdp', 'tp'), may hold values from -2.5 to 2.5
- positions: int32 [1024], P('fsdp'), may hold values from 0 to 1023, as said below
- key_quant: bfloat16 [8704, 1024], P('fsdp', 'tp'), may hold values from -4 to 4
- key_scales: float32 [8704, 8], P('fsdp', 'tp'), may hold values from 0.01 to 0.1
- block_counts: int32 [8], replicated, may hold values from 960 to 1088, as said below
Outputs:
- weight_grad: bfloat16 [8704, 1024], P('fsdp', 'tp')
- input_grad: bfloat16 [1024, 8192], P('fsdp', 'tp')
Inputs may be any that keep to these rules, and one draw needn't show every extreme that they name: Index f of fsdp owns the consecutive projection rows from block_counts[0] + ... + block_counts[f-1] on, in its first block_counts[f] slots; the counts sum to 8192, and some index owns exactly 1088 rows. positions count the tokens from the start of their packed document; the first token's document may have begun before the first token, and a document may go on into the next index's tokens.
All inputs are finite; a program needn't handle non-finite values.
Results may differ from a plain program's by a relative error of at most 0.013.
Values may be sent and summed in bfloat16 or wider, within the bound.
A program may use at most 64 MiB of HBM per device.

v0:
```python
import math

import jax
import jax.numpy as jnp
from jax import lax
from jax.sharding import PartitionSpec as P

HD = 128


rope_base = 500000.0


def rotary_backward(key_grad, positions):
    tokens_here = key_grad.shape[0]
    half_dim = HD // 2
    cotangent = key_grad.astype(jnp.float32).reshape(tokens_here, -1, HD)
    freq_idx = jnp.arange(half_dim, dtype=jnp.float32)
    inverse = jnp.exp(-(2.0 * freq_idx / HD) * math.log(rope_base))
    angles = positions.astype(jnp.float32)[:, None] * inverse[None, :]
    cosine = jnp.cos(angles)[:, None, :]
    sine_part = jnp.sin(angles)[:, None, :]
    lower_half = cotangent[..., :half_dim]
    upper_half = cotangent[..., half_dim:]
    back_lower = lower_half * cosine + upper_half * sine_part
    back_upper = upper_half * cosine - lower_half * sine_part
    joined = jnp.concatenate([back_lower, back_upper], axis=-1)
    return joined.reshape(tokens_here, -1).astype(jnp.bfloat16)


def slot_tables(block_counts, slot_count, row_total):
    offsets = jnp.cumsum(block_counts) - block_counts
    owners_n = block_counts.shape[0]
    slot_ids = jnp.arange(owners_n * slot_count, dtype=jnp.int32)
    within = slot_ids % slot_count
    live_counts = jnp.broadcast_to(block_counts[:, None], (owners_n, slot_count)).reshape(-1)
    base_rows = jnp.broadcast_to(offsets[:, None], (owners_n, slot_count)).reshape(-1)
    is_live = within < live_counts
    row_of_slot = jnp.where(is_live, base_rows + within, 0)
    row_ids = jnp.arange(row_total, dtype=jnp.int32)
    at_or_after = row_ids[:, None] >= offsets[None, :]
    owner_of_row = jnp.sum(at_or_after.astype(jnp.int32), axis=1) - 1
    row_begin = jnp.max(jnp.where(at_or_after, offsets[None, :], 0), axis=1)
    slot_of_row = owner_of_row * slot_count + row_ids - row_begin
    return (row_of_slot, is_live, slot_of_row)


def per_device(hidden_in, key_grad, positions, key_quant, key_scales, block_counts):
    slot_count = key_quant.shape[0]
    local_heads = key_scales.shape[1]
    row_total = hidden_in.shape[1]
    row_of_slot, is_live, slot_of_row = slot_tables(block_counts, slot_count, row_total)
    scaled = (
        key_quant.astype(jnp.float32).reshape(slot_count, local_heads, HD) * key_scales[:, :, None]
    )
    local_weights = scaled.astype(jnp.bfloat16).reshape(slot_count, local_heads * HD)
    rotated = rotary_backward(key_grad, positions)
    picked = jnp.where(
        is_live[None, :], jnp.take(hidden_in, row_of_slot, axis=1), jnp.zeros((), jnp.bfloat16)
    )
    weight_grad = lax.psum_scatter(
        lax.dot_general(
            picked, rotated, (((0,), (0,)), ((), ())), preferred_element_type=jnp.float32
        ),
        "fsdp",
        scatter_dimension=0,
        tiled=True,
    ).astype(jnp.bfloat16)
    group_total = lax.axis_size("tp")
    whole_slots = lax.all_gather(local_weights, "fsdp", axis=0, tiled=True)
    ordered = jnp.take(whole_slots, slot_of_row, axis=0)
    own_rows = lax.all_to_all(ordered, "tp", split_axis=0, concat_axis=1, tiled=True)
    all_heads = lax.all_gather(rotated, "tp", axis=1, tiled=True)
    tokens_here = all_heads.shape[0]
    feature_here = own_rows.shape[0]
    heads_grouped = all_heads.reshape(tokens_here, group_total, -1)
    rows_grouped = own_rows.reshape(feature_here, group_total, -1)
    group_part = jnp.einsum(
        "tgk,dgk->gtd", heads_grouped, rows_grouped, preferred_element_type=jnp.float32
    ).astype(jnp.bfloat16)
    input_grad = jnp.sum(group_part.astype(jnp.float32), axis=0).astype(jnp.bfloat16)
    return (weight_grad, input_grad)


def solution(mesh):
    in_specs = (P("fsdp", None), P("fsdp", "tp"), P("fsdp"), P("fsdp", "tp"), P("fsdp", "tp"), P())
    out_specs = (P("fsdp", "tp"), P("fsdp", "tp"))
    return jax.shard_map(
        per_device, mesh=mesh, in_specs=in_specs, out_specs=out_specs, check_vma=False
    )
```

profile of v0, /device:TPU:0, one launch (start us, length us, event | category | flops | bytes accessed | tf_op | source)
XLA Modules:
  0.0 256.9 jit_solution(10514191697717490936)
XLA Ops:
  7.2 0.0 copy-start
  7.2 0.0 all-gather.2.cloned.1.call-start
  7.2 1.0 copy.18
  8.2 0.0 copy-start.2
  8.2 0.0 copy-start.1
  8.2 0.0 copy-start.3
  8.2 2.5 mul.108
  10.8 0.0 copy-done
  10.8 0.9 fusion.13
  11.7 0.0 all-gather.2.cloned.1.call-update
  11.7 0.0 reduce-scatter.2.cloned.1.call-start
  11.8 0.0 copy-done.2
  11.8 0.2 reduce-window.9
  12.0 0.1 broadcast_in_dim.67
  12.1 0.1 reshape.253
  12.2 0.1 reshape.251
  12.2 0.1 broadcast_in_dim.65
  12.3 0.1 reshape.252
  12.4 0.1 reshape.248
  12.5 0.0 copy-done.1
  12.5 0.1 copy.21
  12.6 0.0 copy-done.3
  12.6 3.2 %copy.15 = bf16[128,8192]{0,1:T(8,128)(2,1)S(1)} copy(bf16[128,8192]{1,0:T(8,128)(2,1)} %param.6) | data formatting | bytes 4194304 | tf_op args[0]
  15.9 0.2 fusion.20
  16.1 18.3 %gather_fusion = bf16[8704,128]{1,0:T(8,128)(2,1)} fusion(bf16[128,8192]{0,1:T(8,128)(2,1)S(1)} %copy.15, s32[9216]{0:T(1024)S(1)} %pad_clamp_fusion), kind=kCustom, calls=%fused_computation | custom fusion | bytes 4491264 | tf_op jit(solution)/shard_map/jit(_take)/gather | solution.py:59
  34.4 0.2 multiply_cosine_fusion
  34.7 8.8 %fusion.5 = f32[8704,256]{1,0:T(8,128)} fusion(bf16[128,256]{0,1:T(8,128)(2,1)S(1)} %bitcast.27, bf16[8704,128]{1,0:T(8,128)(2,1)} %gather_fusion, pred[8704]{0:T(1024)(128)(4,1)S(1)} %get-tuple-element.5, pred[8704]{0:T(1024)(128)(4,1)S(1)} %get-tuple-element.4), kind=kOutput, calls=%fused_computation.6 | convolution fusion | flops 572653568 | bytes 11224064 | tf_op jit(solution)/shard_map/dot_general | solution.py:62
  43.5 0.0 reduce-scatter.2.cloned.1.call-update
  43.5 0.3 convert_reduce_fusion
  43.9 0.1 compare_select_fusion.1
  44.0 46.7 %all-gather.2.cloned.1.call-done = bf16[8704,256]{1,0:T(8,128)(2,1)} async-done(((bf16[1088,256]{1,0:T(8,128)(2,1)}), bf16[8704,256]{1,0:T(8,128)(2,1)}) %all-gather.2.cloned.1.call-update) | async-done | bytes 4456464 | tf_op jit(solution)/shard_map/all_gather | solution.py:70
  90.7 33.7 %gather_fusion.1 = bf16[8192,256]{1,0:T(8,128)(2,1)} fusion(bf16[8704,256]{1,0:T(8,128)(2,1)} %all-gather.2.cloned.1.call-done, s32[8192]{0:T(1024)S(1)} %broadcast_clamp_fusion), kind=kCustom, calls=%fused_computation.1 | custom fusion | bytes 8421376 | tf_op jit(solution)/shard_map/jit(_take)/gather | solution.py:71
  124.4 5.3 %broadcast_select_fusion = bf16[4,2048,256]{2,1,0:T(8,128)(2,1)} fusion(bf16[4,2048,256]{2,1,0:T(8,128)(2,1)} %bitcast.24, pred[4,2048]{1,0:T(4,128)(4,1)S(1)} %compare_and_fusion.1), kind=kLoop, calls=%fused_computation.4 | loop fusion | flops 2097152 | bytes 8396800 | tf_op jit(solution)/shard_map/jit(_take)/select_n | solution.py:71
  129.7 4.9 %all-to-all-start = ((bf16[4,2048,256]{2,1,0:T(8,128)(2,1)}), bf16[4,2048,256]{2,1,0:T(8,128)(2,1)}, u32[]{:S(2)}, u32[]{:S(2)}) async-start(bf16[4,2048,256]{2,1,0:T(8,128)(2,1)} %broadcast_select_fusion), calls=%async_computation.1 | async-start | bytes 8388608 | tf_op jit(solution)/shard_map/all_to_all | solution.py:72
  134.6 50.3 %all_gather.6 = bf16[128,1024]{0,1:T(8,128)(2,1)S(1)} all-gather(bf16[128,256]{0,1:T(8,128)(2,1)S(1)} %bitcast.28), channel_id=1, replica_groups=mesh['fsdp'=8,'tp'=4] {'tp'}, dimensions={1}, use_global_device_ids=true | all-gather | bytes 327680 | tf_op jit(solution)/shard_map/all_gather | solution.py:73
  184.9 0.0 all-to-all-done
  184.9 4.8 %fusion.10 = bf16[128,2048]{1,0:T(8,128)(2,1)} fusion(bf16[128,4,256]{0,2,1:T(8,128)(2,1)S(1)} %bitcast.26, bf16[4,2048,256]{2,1,0:T(8,128)(2,1)} %all-to-all-done), kind=kOutput, calls=%fused_computation.11 | convolution fusion | flops 538705920 | bytes 4980736 | tf_op jit(solution)/shard_map/tgk,dgk->gtd/dot_general | solution.py:78
  189.7 58.2 %reduce-scatter.2.cloned.1.call-done = f32[1088,256]{1,0:T(8,128)} async-done(((f32[8704,256]{1,0:T(8,128)}), f32[1088,256]{1,0:T(8,128)}) %reduce-scatter.2.cloned.1.call-update) | async-done | bytes 1114128 | tf_op jit(solution)/shard_map/reduce_scatter | solution.py:61
  248.0 2.1 convert_element_type.28
  (12 shorter events, 0.2 us)
Async XLA Ops:
  7.2 3.6 %copy-start = (bf16[1088,256]{1,0:T(8,128)(2,1)S(1)}, bf16[1088,256]{1,0:T(8,128)(2,1)}, u32[]{:S(2)}) copy-start(bf16[1088,256]{1,0:T(8,128)(2,1)} %param.9) | copy-start | bytes 1671172
  7.2 83.5 %all-gather.2.cloned.1.call-start = ((), (), s32[]{:S(2)}) async-start(), calls=%async_computation.3 | async-start | bytes 5013504 | tf_op jit(solution)/shard_map/all_gather | solution.py:70
  8.2 3.6 %copy-start.2 = (s32[8]{0:T(128)S(1)}, s32[8]{0:T(128)}, u32[]{:S(2)}) copy-start(s32[8]{0:T(128)} %param.11) | copy-start | bytes 100
  8.2 4.3 %copy-start.1 = (bf16[128,256]{1,0:T(8,128)(2,1)S(1)}, bf16[128,256]{1,0:T(8,128)(2,1)}, u32[]{:S(2)}) copy-start(bf16[128,256]{1,0:T(8,128)(2,1)} %param.7) | copy-start | bytes 196612
  8.2 4.4 %copy-start.3 = (s32[128]{0:T(128)S(1)}, s32[128]{0:T(128)}, u32[]{:S(2)}) copy-start(s32[128]{0:T(128)} %param.8) | copy-start | bytes 1540
  11.7 236.3 %reduce-scatter.2.cloned.1.call-start = ((), (), s32[]{:S(2)}) async-start(), calls=%async_computation.2 | async-start | bytes 10027008 | tf_op jit(solution)/shard_map/reduce_scatter | solution.py:61
  129.7 55.2 %all-to-all-start = ((bf16[4,2048,256]{2,1,0:T(8,128)(2,1)}), bf16[4,2048,256]{2,1,0:T(8,128)(2,1)}, u32[]{:S(2)}, u32[]{:S(2)}) async-start(bf16[4,2048,256]{2,1,0:T(8,128)(2,1)} %broadcast_select_fusion), calls=%async_computation.1 | async-start | bytes 8388608 | tf_op jit(solution)/shard_map/all_to_all | solution.py:72
Sparse Core Ops, SparseCore 0:
  11.9 78.7 all-gather.1
  94.3 153.6 reduce-scatter.1
where the time goes:
time: 258 us; the launch traced here: 257 us
  waiting for transfers between devices  105 us (41%)
  local copies, waits for them, and re-layouts  59.4 us (23%)
  blocking collectives  50.3 us (19%)
  between operations  14.2 us (6%)
  matrix products  13.6 us (5%)
  other arithmetic  9.44 us (4%)
  starting transfers between devices  4.98 us (2%)
    reduce_scatter x1, waiting for transfers between devices, per_device(): lax.psum_scatter(lax.dot_general(picked, rotated, (((0,), (0,)), ((), ())...  58.2 us
    all_gather x1, blocking collectives, per_device(): all_heads = lax.all_gather(rotated, 'tp', axis=1, tiled=True)  50.3 us
    all_gather x1, waiting for transfers between devices, per_device(): whole_slots = lax.all_gather(local_weights, 'fsdp', axis=0, tiled=True)  46.7 us
    gather x1, local copies, waits for them, and re-layouts, per_device(): ordered = jnp.take(whole_slots, slot_of_row, axis=0)  33.7 us
    gather x1, local copies, waits for them, and re-layouts, per_device(): jnp.take(hidden_in, row_of_slot, axis=1)  18.3 us
    dot_general x1, matrix products, per_device(): lax.dot_general(picked, rotated, (((0,), (0,)), ((), ())), preferred_elem...  8.82 us
    select_n x2, other arithmetic, per_device(): ordered = jnp.take(whole_slots, slot_of_row, axis=0)  5.34 us
  transfers between devices with their start and end apart: 3, of which 2 were waited for; matrix products, arithmetic and copies ran while one was open for 30% of the time, Pallas kernels for 0%

commit v1 on v0

--- a/solution.py
+++ b/solution.py
@@ -1,14 +1,461 @@
+import functools
 import math
 
 import jax
 import jax.numpy as jnp
 from jax import lax
+from jax.experimental import pallas as pl
+from jax.experimental.pallas import tpu as pltpu
 from jax.sharding import PartitionSpec as P
 
 HD = 128
-
+LANES = 128
+LINE = 2
+MESH = pl.DeviceIdType.MESH
 
 rope_base = 500000.0
+
+
+def rotary_tables(positions):
+    half_dim = HD // 2
+    freq_idx = jnp.arange(half_dim, dtype=jnp.float32)
+    inverse = jnp.exp(-(2.0 * freq_idx / HD) * math.log(rope_base))
+    angles = positions.astype(jnp.float32)[:, None] * inverse[None, :]
+    return jnp.cos(angles), jnp.sin(angles)
+
+
+def offset_range(index, owners_n, row_total, slot_count):
+    least_count = 2 * row_total // owners_n - slot_count
+    later = owners_n - index
+    least = max(index * least_count, row_total - later * slot_count)
+    greatest = min(index * slot_count, row_total - later * least_count)
+    return least, greatest
+
+
+def exchange_fits(owners_n, group_total, slot_count, row_total, tokens_here, width):
+    if group_total % 2 or owners_n % group_total or owners_n % LINE or slot_count % (16 * group_total):
+        return False
+    if tokens_here % LANES or width % LANES or row_total % group_total or (row_total // group_total) % LANES:
+        return False
+    quarter = slot_count // group_total
+    chunk = row_total // group_total
+    per_chunk = owners_n // group_total
+    if 2 * row_total // owners_n - slot_count < quarter or row_total < 2 * quarter + 4 * LANES:
+        return False
+    for owner in range(owners_n):
+        least, greatest = offset_range(owner, owners_n, row_total, slot_count)
+        home = owner // per_chunk
+        for part in range(group_total):
+            reach = range(
+                max(0, (least + part * quarter) // chunk),
+                min(group_total - 1, (greatest + (part + 1) * quarter - 1) // chunk) + 1,
+            )
+            allowed = {home}
+            if part == 0 and owner % per_chunk == 0:
+                allowed.add(home - 1)
+            if part == group_total - 1 and owner % per_chunk == per_chunk - 1:
+                allowed.add(home + 1)
+            if not set(reach) <= allowed:
+                return False
+    return True
+
+
+def prepare_kernel(
+    owners_n, group_total, span, counts_ref, hidden_ref, grad_ref, cos_ref, sin_ref, quant_ref, scales_ref,
+    rot_ref, weights_ref, picked_ref, shifted
+):
+    part = lax.axis_index("tp")
+    row_total = hidden_ref.shape[1]
+    quarter = picked_ref.shape[1]
+    heads = scales_ref.shape[1]
+    cosine = jnp.concatenate([cos_ref[...], cos_ref[...]], axis=1)
+    sine = jnp.concatenate([sin_ref[...], -sin_ref[...]], axis=1)
+    for head in range(heads):
+        cols = pl.ds(head * HD, HD)
+        values = grad_ref[:, cols].astype(jnp.float32)
+        swapped = jnp.concatenate([values[:, HD // 2 :], values[:, : HD // 2]], axis=1)
+        rot_ref[:, cols] = (values * cosine + swapped * sine).astype(jnp.bfloat16)
+        scale = scales_ref[:, head : head + 1]
+        weights_ref[:, cols] = (quant_ref[:, cols].astype(jnp.float32) * scale).astype(jnp.bfloat16)
+    offset = jnp.int32(0)
+    for owner in range(owners_n):
+        count = counts_ref[owner]
+        begin = jnp.minimum(offset + part * quarter, row_total)
+        base = jnp.minimum((begin // LANES) * LANES, row_total - span)
+        window = hidden_ref[:, pl.ds(pl.multiple_of(base, LANES), span)].astype(jnp.float32)
+        buffer = shifted.at[owner % 2]
+        buffer[pl.ds(0, span), :] = window.T
+        moved = buffer[pl.ds(begin - base, quarter), :]
+        slot = lax.broadcasted_iota(jnp.int32, moved.shape, 0) + part * quarter
+        picked_ref[owner] = jnp.where(slot < count, moved, 0.0).astype(jnp.bfloat16)
+        offset = offset + count
+
+
+def assemble_kernel(owners_n, group_total, pad, counts_ref, pieces_ref, out_ref, rows):
+    chunk_at = lax.axis_index("tp")
+    chunk = out_ref.shape[1]
+    quarter = pieces_ref.shape[1]
+    per_chunk = owners_n // group_total
+    offsets = []
+    offset = jnp.int32(0)
+    for owner in range(owners_n):
+        offsets.append(offset)
+        offset = offset + counts_ref[owner]
+
+    def first_row(owner):
+        found = jnp.int32(0)
+        for candidate in range(owners_n):
+            found = jnp.where(owner == candidate, offsets[candidate], found)
+        return found
+
+    limit = rows.shape[0] - quarter
+
+    def place(index, begin):
+        rows[pl.ds(jnp.clip(begin, 0, limit), quarter), :] = pieces_ref[index].astype(jnp.float32)
+
+    origin = pad - chunk_at * chunk
+    first = chunk_at * per_chunk
+    below = first_row(first - 1) + (group_total - 1) * quarter + origin
+    place(0, jnp.where(chunk_at > 0, below, 0))
+    for near in range(per_chunk):
+        start = first_row(first + near) + origin
+        for part in range(group_total):
+            place(1 + near * group_total + part, start + part * quarter)
+    above = first_row(first + per_chunk) + origin
+    last = 1 + per_chunk * group_total
+    place(last, jnp.where(chunk_at < group_total - 1, above, limit))
+    for at in range(0, chunk, LANES):
+        out_ref[:, pl.ds(at, LANES)] = rows[pl.ds(pad + at, LANES), :].T.astype(jnp.bfloat16)
+
+
+def exchange_kernel(
+    owners_n, group_total, rot_ref, weights_ref, picked_ref, grad_out, pieces_out,
+    rotated, weights, hidden, outgoing, grad_send,
+    own_sem, tp_send, tp_recv, w_send, w_recv, h_send, h_recv,
+    up_send, down_send, side_send, pair_send, net_recv, pair_recv,
+    o_send, e_send, o_recv, g_send, g_recv, local_sem,
+):
+    here = lax.axis_index("fsdp")
+    part = lax.axis_index("tp")
+    core = lax.rem(part, 2)
+    partner = part + 1 - 2 * core
+    tokens, width = rot_ref.shape
+    quarter = picked_ref.shape[1]
+    half = width * group_total // 2
+    depth = owners_n // LINE
+    z = here // LINE
+    y = lax.rem(here, LINE)
+    beside = z * LINE + (1 - y)
+    per_chunk = owners_n // group_total
+    home = here // per_chunk
+    last_piece = 1 + per_chunk * group_total
+
+    def remote(src, dst, send, recv, where):
+        return pltpu.make_async_remote_copy(
+            src_ref=src, dst_ref=dst, send_sem=send, recv_sem=recv, device_id=where, device_id_type=MESH
+        )
+
+    def rows_of(owner):
+        return pl.ds(pl.multiple_of(owner * tokens, tokens), tokens)
+
+    def cols_of(group):
+        return pl.ds(pl.multiple_of(group * width, width), width)
+
+    def slots_of(group):
+        return pl.ds(pl.multiple_of(group * quarter, 16), quarter)
+
+    def spread(step):
+        target = lax.rem(part + step, group_total)
+        block = rotated.at[rows_of(here), cols_of(part)]
+        return remote(rot_ref, block, tp_send.at[step - 1], tp_recv.at[step - 1], (here, target))
+
+    def weigh(step):
+        target = lax.rem(part + step, group_total)
+        return remote(
+            weights_ref.at[slots_of(target), :], weights.at[:, cols_of(part)],
+            w_send.at[step - 1], w_recv.at[step - 1], (here, target),
+        )
+
+    def hide(step):
+        target = lax.rem(here + step, owners_n)
+        return remote(
+            picked_ref.at[target], hidden.at[:, rows_of(here)],
+            h_send.at[step - 1], h_recv.at[step - 1], (target, part),
+        )
+
+    def relay(owner, send, where):
+        view = rotated.at[rows_of(owner), pl.ds(pl.multiple_of(core * half, half), half)]
+        return remote(view, view, send.at[owner], net_recv.at[owner], (where, part))
+
+    def share(owner):
+        view = rotated.at[rows_of(owner), pl.ds(pl.multiple_of(core * half, half), half)]
+        return remote(view, view, pair_send.at[owner], pair_recv.at[owner], (here, partner))
+
+    own_rot = pltpu.make_async_copy(rot_ref, rotated.at[rows_of(here), cols_of(part)], own_sem.at[0])
+    own_weights = pltpu.make_async_copy(
+        weights_ref.at[slots_of(part), :], weights.at[:, cols_of(part)], own_sem.at[1]
+    )
+    own_hidden = pltpu.make_async_copy(picked_ref.at[here], hidden.at[:, rows_of(here)], own_sem.at[2])
+    own_rot.start()
+    own_weights.start()
+    own_hidden.start()
+    for step in range(1, group_total):
+        spread(step).start()
+    for step in range(1, group_total):
+        weigh(step).start()
+    own_rot.wait()
+    for step in range(1, group_total):
+        spread(step).wait_recv()
+
+    below, above = here - LINE, here + LINE
+
+    def travel(owner, go_up, go_down, act):
+        @pl.when(go_up)
+        def _():
+            act(relay(owner, up_send, above))
+
+        @pl.when(go_down)
+        def _():
+            act(relay(owner, down_send, below))
+
+    def begin(copy):
+        copy.start()
+
+    def finish(copy):
+        copy.wait_send()
+
+    travel(here, z < depth - 1, z > 0, begin)
+    relay(here, side_send, beside).start()
+    for away in range(1, depth + 1):
+        for sign in (-1, 1):
+            if away < depth:
+                level = z + sign * away
+                owner = level * LINE + y
+
+                @pl.when((level >= 0) & (level < depth))
+                def _():
+                    relay(owner, up_send, here).wait_recv()
+                    if sign < 0:
+                        travel(owner, z < depth - 1, z < 0, begin)
+                    else:
+                        travel(owner, z < 0, z > 0, begin)
+                    relay(owner, side_send, beside).start()
+                    share(owner).start()
+
+            if away > 1 or sign < 0:
+                level_near = z + sign * (away - 1)
+                other = level_near * LINE + (1 - y)
+
+                @pl.when((level_near >= 0) & (level_near < depth))
+                def _():
+                    relay(other, up_send, here).wait_recv()
+                    share(other).start()
+
+    for step in range(1, owners_n):
+        hide(step).start()
+
+    own_weights.wait()
+    for step in range(1, group_total):
+        weigh(step).wait_recv()
+
+    def send_piece(owner, act_remote, act_local):
+        source = outgoing.at[owner]
+
+        def give(to_chunk, index, send, slot):
+            mine = (owner == here) & (to_chunk == part)
+
+            @pl.when(jnp.logical_not(mine))
+            def _():
+                act_remote(remote(source, pieces_out.at[index], send, o_recv.at[index], (owner, to_chunk)))
+
+            @pl.when(mine)
+            def _():
+                act_local(pltpu.make_async_copy(source, pieces_out.at[index], local_sem.at[slot]))
+
+        near = lax.rem(here, per_chunk)
+        give(home, 1 + near * group_total + part, o_send.at[owner], 0)
+
+        @pl.when((near == per_chunk - 1) & (part == group_total - 1) & (home < group_total - 1))
+        def _():
+            give(home + 1, 0, e_send.at[owner], 1)
+
+        @pl.when((near == 0) & (part == 0) & (home > 0))
+        def _():
+            give(home - 1, last_piece, e_send.at[owner], 1)
+
+    def nothing(copy):
+        pass
+
+    def produce(step, carry):
+        owner = lax.rem(here + step, owners_n)
+
+        @pl.when(step > 0)
+        def _():
+            share(owner).wait_recv()
+
+        outgoing[owner] = lax.dot_general(
+            weights[...], rotated[rows_of(owner), :], (((1,), (1,)), ((), ())),
+            preferred_element_type=jnp.float32,
+        ).astype(jnp.bfloat16)
+
+        @pl.when(step > 0)
+        def _():
+            send_piece(lax.rem(here + step - 1, owners_n), begin, begin)
+
+        return carry
+
+    lax.fori_loop(0, owners_n, produce, 0)
+    send_piece(lax.rem(here + owners_n - 1, owners_n), begin, begin)
+
+    own_hidden.wait()
+    for step in range(1, owners_n):
+        hide(step).wait_recv()
+
+    def send_grad(step):
+        target = lax.rem(part + step, group_total)
+        return remote(
+            grad_send.at[target], grad_out.at[part], g_send.at[step - 1], g_recv.at[step - 1], (here, target)
+        )
+
+    def reduce(step, carry):
+        target = lax.rem(part + step, group_total)
+        grad_send[target] = jnp.dot(
+            hidden[...], rotated[:, cols_of(target)], preferred_element_type=jnp.float32
+        ).astype(jnp.bfloat16)
+
+        @pl.when(step > 1)
+        def _():
+            send_grad(step - 1).start()
+
+        return carry
+
+    lax.fori_loop(1, group_total + 1, reduce, 0)
+    own_grad = pltpu.make_async_copy(grad_send.at[part], grad_out.at[part], own_sem.at[3])
+    own_grad.start()
+
+    for owner in range(owners_n):
+        send_piece(jnp.int32(owner), finish, lambda copy: copy.wait())
+    for near in range(per_chunk):
+        for source in range(group_total):
+            index = 1 + near * group_total + source
+
+            @pl.when(jnp.logical_not((home == part) & (here == part * per_chunk + near) & (part == source)))
+            def _():
+                remote(outgoing.at[0], pieces_out.at[index], o_send.at[0], o_recv.at[index], (here, partner)).wait_recv()
+
+    for index, exists, mine in (
+        (0, part > 0, (here == part * per_chunk - 1) & (part == group_total - 1)),
+        (last_piece, part < group_total - 1, (here == (part + 1) * per_chunk) & (part == 0)),
+    ):
+
+        @pl.when(exists & jnp.logical_not(mine))
+        def _():
+            remote(outgoing.at[0], pieces_out.at[index], o_send.at[0], o_recv.at[index], (here, partner)).wait_recv()
+
+    own_grad.wait()
+    for step in range(1, group_total):
+        send_grad(step).wait_send()
+        remote(grad_send.at[0], grad_out.at[0], g_send.at[step - 1], g_recv.at[step - 1], (here, partner)).wait_recv()
+    for step in range(1, group_total):
+        spread(step).wait_send()
+        weigh(step).wait_send()
+    for step in range(1, owners_n):
+        hide(step).wait_send()
+    travel(here, z < depth - 1, z > 0, finish)
+    relay(here, side_send, beside).wait_send()
+    for away in range(1, depth):
+        for sign in (-1, 1):
+            level = z + sign * away
+            owner = level * LINE + y
+
+            @pl.when((level >= 0) & (level < depth))
+            def _():
+                if sign < 0:
+                    travel(owner, z < depth - 1, z < 0, finish)
+                else:
+                    travel(owner, z < 0, z > 0, finish)
+                relay(owner, side_send, beside).wait_send()
+
+    def drain(step, carry):
+        share(lax.rem(here + step, owners_n)).wait_send()
+        return carry
+
+    lax.fori_loop(1, owners_n, drain, 0)
+
+
+def exchange_plan(hidden_in, key_grad, positions, key_quant, key_scales, block_counts):
+    owners_n = lax.axis_size("fsdp")
+    group_total = lax.axis_size("tp")
+    slot_count, width = key_quant.shape
+    tokens_here, row_total = hidden_in.shape
+    quarter = slot_count // group_total
+    chunk = row_total // group_total
+    per_chunk = owners_n // group_total
+    columns = width * group_total
+    vmem = pl.BlockSpec(memory_space=pltpu.VMEM)
+    smem = pl.BlockSpec(memory_space=pltpu.SMEM)
+    span = -(-(quarter + LANES) // LANES) * LANES
+    cosine, sine = rotary_tables(positions)
+    rot, local_weights, picked = pl.pallas_call(
+        functools.partial(prepare_kernel, owners_n, group_total, span),
+        out_shape=(
+            jax.ShapeDtypeStruct((tokens_here, width), jnp.bfloat16),
+            jax.ShapeDtypeStruct((slot_count, width), jnp.bfloat16),
+            jax.ShapeDtypeStruct((owners_n, quarter, tokens_here), jnp.bfloat16),
+        ),
+        in_specs=[smem] + [vmem] * 6,
+        out_specs=(vmem,) * 3,
+        scratch_shapes=[pltpu.VMEM((2, 2 * span + quarter, tokens_here), jnp.float32)],
+        name="prepare",
+    )(block_counts, hidden_in, key_grad, cosine, sine, key_quant, key_scales)
+
+    pieces_n = 2 + per_chunk * group_total
+    dma = pltpu.SemaphoreType.DMA
+    weight_grad, pieces = pl.pallas_call(
+        functools.partial(exchange_kernel, owners_n, group_total),
+        out_shape=(
+            jax.ShapeDtypeStruct((group_total, quarter, width), jnp.bfloat16),
+            jax.ShapeDtypeStruct((pieces_n, quarter, tokens_here), jnp.bfloat16),
+        ),
+        in_specs=[vmem] * 3,
+        out_specs=(vmem,) * 2,
+        scratch_shapes=[
+            pltpu.VMEM((owners_n * tokens_here, columns), jnp.bfloat16),
+            pltpu.VMEM((quarter, columns), jnp.bfloat16),
+            pltpu.VMEM((quarter, owners_n * tokens_here), jnp.bfloat16),
+            pltpu.VMEM((owners_n, quarter, tokens_here), jnp.bfloat16),
+            pltpu.VMEM((group_total, quarter, width), jnp.bfloat16),
+            dma((4,)),
+            dma((group_total - 1,)), dma((group_total - 1,)),
+            dma((group_total - 1,)), dma((group_total - 1,)),
+            dma((owners_n - 1,)), dma((owners_n - 1,)),
+            dma((owners_n,)), dma((owners_n,)), dma((owners_n,)), dma((owners_n,)),
+            dma((owners_n,)), dma((owners_n,)),
+            dma((owners_n,)), dma((owners_n,)), dma((pieces_n,)),
+            dma((group_total - 1,)), dma((group_total - 1,)),
+            dma((2,)),
+        ],
+        compiler_params=pltpu.CompilerParams(has_side_effects=True),
+        name="exchange",
+    )(rot, local_weights, picked)
+
+    margin = max(
+        max(
+            chunk * (owner // per_chunk) - offset_range(owner - 1, owners_n, row_total, slot_count)[0]
+            for owner in range(per_chunk, owners_n, per_chunk)
+        ),
+        2 * quarter,
+    ) if group_total > 1 else 2 * quarter
+    pad = -(-(margin + slot_count) // 8) * 8
+    input_grad = pl.pallas_call(
+        functools.partial(assemble_kernel, owners_n, group_total, pad),
+        out_shape=jax.ShapeDtypeStruct((tokens_here, chunk), jnp.bfloat16),
+        in_specs=[smem, vmem],
+        out_specs=vmem,
+        scratch_shapes=[pltpu.VMEM((chunk + 2 * pad, tokens_here), jnp.float32)],
+        name="assemble",
+    )(block_counts, pieces)
+    return (weight_grad.reshape(slot_count, width), input_grad)
 
 
 def rotary_backward(key_grad, positions):
@@ -45,7 +492,7 @@
     return (row_of_slot, is_live, slot_of_row)
 
 
-def per_device(hidden_in, key_grad, positions, key_quant, key_scales, block_counts):
+def gather_plan(hidden_in, key_grad, positions, key_quant, key_scales, block_counts):
     slot_count = key_quant.shape[0]
     local_heads = key_scales.shape[1]
     row_total = hidden_in.shape[1]
@@ -82,6 +529,16 @@
     return (weight_grad, input_grad)
 
 
+def per_device(hidden_in, key_grad, positions, key_quant, key_scales, block_counts):
+    tokens_here, row_total = hidden_in.shape
+    slot_count, width = key_quant.shape
+    fits = exchange_fits(
+        lax.axis_size("fsdp"), lax.axis_size("tp"), slot_count, row_total, tokens_here, width
+    )
+    plan = exchange_plan if fits else gather_plan
+    return plan(hidden_in, key_grad, positions, key_quant, key_scales, block_counts)
+
+
 def solution(mesh):
     in_specs = (P("fsdp", None), P("fsdp", "tp"), P("fsdp"), P("fsdp", "tp"), P("fsdp", "tp"), P())
     out_specs = (P("fsdp", "tp"), P("fsdp", "tp"))

time: 258 us -> 73.3 us (0.28)
  the two profiles are of different devices: /device:TPU:0 before, /device:TPU:13 now
where the time goes in v1:
time: 73.3 us; the launch traced here: 73 us
  Pallas kernels  67.1 us (92%)
  local copies, waits for them, and re-layouts  3.63 us (5%)
  other arithmetic  1.62 us (2%)
    pallas_call x1, Pallas kernels, exchange_plan(): pl.pallas_call(functools.partial(exchange_kernel, owners_n, group_total),...  61.3 us
    unnamed x2, local copies, waits for them, and re-layouts  3.63 us
    pallas_call x1, Pallas kernels, exchange_plan(): pl.pallas_call(functools.partial(prepare_kernel, owners_n, group_total, s...  3.57 us
    pallas_call x1, Pallas kernels, exchange_plan(): pl.pallas_call(functools.partial(assemble_kernel, owners_n, group_total,...  2.22 us

profile of v1, /device:TPU:13, one launch (start us, length us, event | category | flops | bytes accessed | tf_op | source)
XLA Modules:
  0.0 73.0 jit_solution(7481613076049789197)
XLA Ops:
  0.6 0.7 convert_element_type.3
  1.3 0.9 %multiply_sine_fusion = (f32[128,64]{1,0:T(8,128)}, f32[128,64]{1,0:T(8,128)}) fusion(f32[64]{0:T(128)S(1)} %multiply_exponential_fusion, f32[128]{0:T(128)S(1)} %convert_element_type.3), kind=kLoop, calls=%fused_computation | loop fusion | flops 8192 | bytes 66304 | tf_op jit(solution)/shard_map/sin | solution.py:24
  2.2 1.7 %copy.8.scales_ref = f32[1088,2]{1,0:T(8,128)} copy(f32[1088,2]{0,1:T(2,128)} %param.10) | data formatting | bytes 17408 | tf_op args[4]
  4.0 3.6 %prepare.1 = (bf16[128,256]{1,0:T(8,128)(2,1)}, bf16[1088,256]{1,0:T(8,128)(2,1)}, bf16[8,272,128]{2,1,0:T(8,128)(2,1)}) custom-call(s32[8]{0:T(128)} %counts_ref.3, bf16[128,8192]{1,0:T(8,128)(2,1)} %hidden_ref.1, bf16[128,256]{1,0:T(8,128)(2,1)} %grad_ref.1, f32[128,64]{1,0:T(8,128)} %get-tuple-element.13.cos_ref, f32[128,64]{1,0:T(8,128)} %get-tuple-element.12.sin_ref, ...), custom_call_target="tpu_custom_call" | custom-call | tf_op jit(solution)/shard_map/prepare/pallas_call | solution.py:399
  7.6 61.3 %exchange.1 = (bf16[4,272,256]{2,1,0:T(8,128)(2,1)}, bf16[10,272,128]{2,1,0:T(8,128)(2,1)}) custom-call(bf16[128,256]{1,0:T(8,128)(2,1)} %get-tuple-element.7.rot_ref, bf16[1088,256]{1,0:T(8,128)(2,1)} %get-tuple-element.8.weights_ref, bf16[8,272,128]{2,1,0:T(8,128)(2,1)} %get-tuple-element.9.picked_ref), custom_call_target="tpu_custom_call" | custom-call | tf_op jit(solution)/shard_map/exchange/pallas_call | solution.py:414
  68.9 2.2 %assemble.1 = bf16[128,2048]{1,0:T(8,128)(2,1)} custom-call(s32[8]{0:T(128)} %counts_ref.3, bf16[10,272,128]{2,1,0:T(8,128)(2,1)} %get-tuple-element.11.pieces_ref), custom_call_target="tpu_custom_call" | custom-call | tf_op jit(solution)/shard_map/assemble/pallas_call | solution.py:450
  71.1 1.9 %copy.10 = bf16[1088,256]{1,0:T(8,128)(2,1)} copy(bf16[1088,256]{1,0:T(8,128)(2,1)} %bitcast.1) | data formatting | bytes 1114112
  (1 shorter events, 0.0 us)

commit v2 on v1

--- a/solution.py
+++ b/solution.py
@@ -60,38 +60,31 @@
     return True
 
 
-def prepare_kernel(
-    owners_n, group_total, span, counts_ref, hidden_ref, grad_ref, cos_ref, sin_ref, quant_ref, scales_ref,
-    rot_ref, weights_ref, picked_ref, shifted
-):
+def pick_kernel(owners_n, group_total, span, counts_ref, hidden_any, picked_ref, windows, shifted, load_sem):
     part = lax.axis_index("tp")
-    row_total = hidden_ref.shape[1]
+    row_total = hidden_any.shape[1]
     quarter = picked_ref.shape[1]
-    heads = scales_ref.shape[1]
-    cosine = jnp.concatenate([cos_ref[...], cos_ref[...]], axis=1)
-    sine = jnp.concatenate([sin_ref[...], -sin_ref[...]], axis=1)
-    for head in range(heads):
-        cols = pl.ds(head * HD, HD)
-        values = grad_ref[:, cols].astype(jnp.float32)
-        swapped = jnp.concatenate([values[:, HD // 2 :], values[:, : HD // 2]], axis=1)
-        rot_ref[:, cols] = (values * cosine + swapped * sine).astype(jnp.bfloat16)
-        scale = scales_ref[:, head : head + 1]
-        weights_ref[:, cols] = (quant_ref[:, cols].astype(jnp.float32) * scale).astype(jnp.bfloat16)
     offset = jnp.int32(0)
+    plans = []
     for owner in range(owners_n):
         count = counts_ref[owner]
-        begin = jnp.minimum(offset + part * quarter, row_total)
-        base = jnp.minimum((begin // LANES) * LANES, row_total - span)
-        window = hidden_ref[:, pl.ds(pl.multiple_of(base, LANES), span)].astype(jnp.float32)
-        buffer = shifted.at[owner % 2]
-        buffer[pl.ds(0, span), :] = window.T
-        moved = buffer[pl.ds(begin - base, quarter), :]
+        start = jnp.minimum(offset + part * quarter, row_total)
+        base = jnp.minimum((start // LANES) * LANES, row_total - span)
+        load = pltpu.make_async_copy(
+            hidden_any.at[:, pl.ds(pl.multiple_of(base, LANES), span)], windows.at[owner], load_sem.at[owner]
+        )
+        load.start()
+        plans.append((count, start - base, load))
+        offset = offset + count
+    for owner, (count, shift, load) in enumerate(plans):
+        load.wait()
+        shifted[owner, pl.ds(0, span), :] = windows[owner].astype(jnp.float32).T
+        moved = shifted[owner, pl.ds(shift, quarter), :]
         slot = lax.broadcasted_iota(jnp.int32, moved.shape, 0) + part * quarter
         picked_ref[owner] = jnp.where(slot < count, moved, 0.0).astype(jnp.bfloat16)
-        offset = offset + count
-
-
-def assemble_kernel(owners_n, group_total, pad, counts_ref, pieces_ref, out_ref, rows):
+
+
+def assemble_kernel(owners_n, group_total, pad, counts_ref, pieces_ref, grad_ref, grad_out, out_ref, rows):
     chunk_at = lax.axis_index("tp")
     chunk = out_ref.shape[1]
     quarter = pieces_ref.shape[1]
@@ -113,6 +106,8 @@
     def place(index, begin):
         rows[pl.ds(jnp.clip(begin, 0, limit), quarter), :] = pieces_ref[index].astype(jnp.float32)
 
+    for part in range(group_total):
+        grad_out[pl.ds(part * quarter, quarter), :] = grad_ref[part]
     origin = pad - chunk_at * chunk
     first = chunk_at * per_chunk
     below = first_row(first - 1) + (group_total - 1) * quarter + origin
@@ -129,7 +124,9 @@
 
 
 def exchange_kernel(
-    owners_n, group_total, rot_ref, weights_ref, picked_ref, grad_out, pieces_out,
+    owners_n, group_total, picked_ref, grad_ref, cos_ref, sin_ref, quant_ref, scales_ref,
+    grad_out, pieces_out,
+    rot_ref, weights_ref,
     rotated, weights, hidden, outgoing, grad_send,
     own_sem, tp_send, tp_recv, w_send, w_recv, h_send, h_recv,
     up_send, down_send, side_send, pair_send, net_recv, pair_recv,
@@ -176,11 +173,16 @@
             w_send.at[step - 1], w_recv.at[step - 1], (here, target),
         )
 
-    def hide(step):
-        target = lax.rem(here + step, owners_n)
+    def hide(target):
         return remote(
             picked_ref.at[target], hidden.at[:, rows_of(here)],
-            h_send.at[step - 1], h_recv.at[step - 1], (target, part),
+            h_send.at[target], h_recv.at[here], (target, part),
+        )
+
+    def hidden_from(owner):
+        return remote(
+            picked_ref.at[owner], hidden.at[:, rows_of(owner)],
+            h_send.at[owner], h_recv.at[owner], (owner, part),
         )
 
     def relay(owner, send, where):
@@ -196,13 +198,35 @@
         weights_ref.at[slots_of(part), :], weights.at[:, cols_of(part)], own_sem.at[1]
     )
     own_hidden = pltpu.make_async_copy(picked_ref.at[here], hidden.at[:, rows_of(here)], own_sem.at[2])
-    own_rot.start()
+    own_hidden.start()
+    heads = scales_ref.shape[0]
+    cosine = jnp.concatenate([cos_ref[...], cos_ref[...]], axis=1)
+    sine = jnp.concatenate([sin_ref[...], -sin_ref[...]], axis=1)
+    for head in range(heads):
+        cols = pl.ds(head * HD, HD)
+        values = grad_ref[:, cols].astype(jnp.float32)
+        swapped = jnp.concatenate([values[:, HD // 2 :], values[:, : HD // 2]], axis=1)
+        rot_ref[:, cols] = (values * cosine + swapped * sine).astype(jnp.bfloat16)
+    for head in range(heads):
+        cols = pl.ds(head * HD, HD)
+        scale = jnp.broadcast_to(scales_ref[head : head + 1, :], (HD, scales_ref.shape[1])).T
+        weights_ref[:, cols] = (quant_ref[:, cols].astype(jnp.float32) * scale).astype(jnp.bfloat16)
+        if head == 0:
+            hide(beside).start()
+            own_rot.start()
+            for step in range(1, group_total):
+                spread(step).start()
     own_weights.start()
-    own_hidden.start()
-    for step in range(1, group_total):
-        spread(step).start()
     for step in range(1, group_total):
         weigh(step).start()
+
+    def hide_at(rise, across):
+        level = z + rise
+
+        @pl.when((level >= 0) & (level < depth))
+        def _():
+            hide(level * LINE + (1 - y if across else y)).start()
+
     own_rot.wait()
     for step in range(1, group_total):
         spread(step).wait_recv()
@@ -224,9 +248,58 @@
     def finish(copy):
         copy.wait_send()
 
+    def send_piece(owner, act_remote, act_local):
+        source = outgoing.at[owner]
+
+        def give(to_chunk, index, send, slot):
+            mine = (owner == here) & (to_chunk == part)
+
+            @pl.when(jnp.logical_not(mine))
+            def _():
+                act_remote(remote(source, pieces_out.at[index], send, o_recv.at[index], (owner, to_chunk)))
+
+            @pl.when(mine)
+            def _():
+                act_local(pltpu.make_async_copy(source, pieces_out.at[index], local_sem.at[slot]))
+
+        near = lax.rem(here, per_chunk)
+        give(home, 1 + near * group_total + part, o_send.at[owner], 0)
+
+        @pl.when((near == per_chunk - 1) & (part == group_total - 1) & (home < group_total - 1))
+        def _():
+            give(home + 1, 0, e_send.at[owner], 1)
+
+        @pl.when((near == 0) & (part == 0) & (home > 0))
+        def _():
+            give(home - 1, last_piece, e_send.at[owner], 1)
+
     travel(here, z < depth - 1, z > 0, begin)
     relay(here, side_send, beside).start()
-    for away in range(1, depth + 1):
+    hide_at(1, False)
+    hide_at(-1, False)
+
+    def produce(owner):
+        outgoing[owner] = lax.dot_general(
+            weights[...], rotated[rows_of(owner), :], (((1,), (1,)), ((), ())),
+            preferred_element_type=jnp.float32,
+        ).astype(jnp.bfloat16)
+
+    own_weights.wait()
+    for step in range(1, group_total):
+        weigh(step).wait_recv()
+    produce(here)
+
+    def stage_items(away):
+        items = []
+        for sign in (-1, 1):
+            if 0 < away < depth:
+                items.append((z + sign * away, y))
+            if away > 1 or (away == 1 and sign < 0):
+                items.append((z + sign * (away - 1), 1 - y))
+        return items
+
+    send_piece(here, begin, begin)
+    for away in range(1, depth + 2):
         for sign in (-1, 1):
             if away < depth:
                 level = z + sign * away
@@ -242,7 +315,7 @@
                     relay(owner, side_send, beside).start()
                     share(owner).start()
 
-            if away > 1 or sign < 0:
+            if away <= depth and (away > 1 or sign < 0):
                 level_near = z + sign * (away - 1)
                 other = level_near * LINE + (1 - y)
 
@@ -251,65 +324,29 @@
                     relay(other, up_send, here).wait_recv()
                     share(other).start()
 
-    for step in range(1, owners_n):
-        hide(step).start()
-
-    own_weights.wait()
-    for step in range(1, group_total):
-        weigh(step).wait_recv()
-
-    def send_piece(owner, act_remote, act_local):
-        source = outgoing.at[owner]
-
-        def give(to_chunk, index, send, slot):
-            mine = (owner == here) & (to_chunk == part)
-
-            @pl.when(jnp.logical_not(mine))
+        if away < depth:
+            hide_at(away, True)
+            hide_at(-away, True)
+        if away + 1 < depth:
+            hide_at(away + 1, False)
+            hide_at(-away - 1, False)
+        ready = stage_items(away - 1)
+        for level, row in ready:
+
+            @pl.when((level >= 0) & (level < depth))
             def _():
-                act_remote(remote(source, pieces_out.at[index], send, o_recv.at[index], (owner, to_chunk)))
-
-            @pl.when(mine)
+                share(level * LINE + row).wait_recv()
+                produce(level * LINE + row)
+
+        for level, row in ready:
+
+            @pl.when((level >= 0) & (level < depth))
             def _():
-                act_local(pltpu.make_async_copy(source, pieces_out.at[index], local_sem.at[slot]))
-
-        near = lax.rem(here, per_chunk)
-        give(home, 1 + near * group_total + part, o_send.at[owner], 0)
-
-        @pl.when((near == per_chunk - 1) & (part == group_total - 1) & (home < group_total - 1))
-        def _():
-            give(home + 1, 0, e_send.at[owner], 1)
-
-        @pl.when((near == 0) & (part == 0) & (home > 0))
-        def _():
-            give(home - 1, last_piece, e_send.at[owner], 1)
-
-    def nothing(copy):
-        pass
-
-    def produce(step, carry):
-        owner = lax.rem(here + step, owners_n)
-
-        @pl.when(step > 0)
-        def _():
-            share(owner).wait_recv()
-
-        outgoing[owner] = lax.dot_general(
-            weights[...], rotated[rows_of(owner), :], (((1,), (1,)), ((), ())),
-            preferred_element_type=jnp.float32,
-        ).astype(jnp.bfloat16)
-
-        @pl.when(step > 0)
-        def _():
-            send_piece(lax.rem(here + step - 1, owners_n), begin, begin)
-
-        return carry
-
-    lax.fori_loop(0, owners_n, produce, 0)
-    send_piece(lax.rem(here + owners_n - 1, owners_n), begin, begin)
+                send_piece(level * LINE + row, begin, begin)
 
     own_hidden.wait()
     for step in range(1, owners_n):
-        hide(step).wait_recv()
+        hidden_from(lax.rem(here + step, owners_n)).wait_recv()
 
     def send_grad(step):
         target = lax.rem(part + step, group_total)
@@ -360,7 +397,7 @@
         spread(step).wait_send()
         weigh(step).wait_send()
     for step in range(1, owners_n):
-        hide(step).wait_send()
+        hide(lax.rem(here + step, owners_n)).wait_send()
     travel(here, z < depth - 1, z > 0, finish)
     relay(here, side_send, beside).wait_send()
     for away in range(1, depth):
@@ -393,21 +430,22 @@
     per_chunk = owners_n // group_total
     columns = width * group_total
     vmem = pl.BlockSpec(memory_space=pltpu.VMEM)
+    anywhere = pl.BlockSpec(memory_space=pl.ANY)
     smem = pl.BlockSpec(memory_space=pltpu.SMEM)
     span = -(-(quarter + LANES) // LANES) * LANES
     cosine, sine = rotary_tables(positions)
-    rot, local_weights, picked = pl.pallas_call(
-        functools.partial(prepare_kernel, owners_n, group_total, span),
-        out_shape=(
-            jax.ShapeDtypeStruct((tokens_here, width), jnp.bfloat16),
-            jax.ShapeDtypeStruct((slot_count, width), jnp.bfloat16),
-            jax.ShapeDtypeStruct((owners_n, quarter, tokens_here), jnp.bfloat16),
-        ),
-        in_specs=[smem] + [vmem] * 6,
-        out_specs=(vmem,) * 3,
-        scratch_shapes=[pltpu.VMEM((2, 2 * span + quarter, tokens_here), jnp.float32)],
-        name="prepare",
-    )(block_counts, hidden_in, key_grad, cosine, sine, key_quant, key_scales)
+    picked = pl.pallas_call(
+        functools.partial(pick_kernel, owners_n, group_total, span),
+        out_shape=jax.ShapeDtypeStruct((owners_n, quarter, tokens_here), jnp.bfloat16),
+        in_specs=[smem, anywhere],
+        out_specs=vmem,
+        scratch_shapes=[
+            pltpu.VMEM((owners_n, tokens_here, span), jnp.bfloat16),
+            pltpu.VMEM((owners_n, 2 * span + quarter, tokens_here), jnp.float32),
+            pltpu.SemaphoreType.DMA((owners_n,)),
+        ],
+        name="pick",
+    )(block_counts, hidden_in)
 
     pieces_n = 2 + per_chunk * group_total
     dma = pltpu.SemaphoreType.DMA
@@ -417,9 +455,11 @@
             jax.ShapeDtypeStruct((group_total, quarter, width), jnp.bfloat16),
             jax.ShapeDtypeStruct((pieces_n, quarter, tokens_here), jnp.bfloat16),
         ),
-        in_specs=[vmem] * 3,
+        in_specs=[vmem] * 6,
         out_specs=(vmem,) * 2,
         scratch_shapes=[
+            pltpu.VMEM((tokens_here, width), jnp.bfloat16),
+            pltpu.VMEM((slot_count, width), jnp.bfloat16),
             pltpu.VMEM((owners_n * tokens_here, columns), jnp.bfloat16),
             pltpu.VMEM((quarter, columns), jnp.bfloat16),
             pltpu.VMEM((quarter, owners_n * tokens_here), jnp.bfloat16),
@@ -428,7 +468,7 @@
             dma((4,)),
             dma((group_total - 1,)), dma((group_total - 1,)),
             dma((group_total - 1,)), dma((group_total - 1,)),
-            dma((owners_n - 1,)), dma((owners_n - 1,)),
+            dma((owners_n,)), dma((owners_n,)),
             dma((owners_n,)), dma((owners_n,)), dma((owners_n,)), dma((owners_n,)),
             dma((owners_n,)), dma((owners_n,)),
             dma((owners_n,)), dma((owners_n,)), dma((pieces_n,)),
@@ -437,7 +477,7 @@
         ],
         compiler_params=pltpu.CompilerParams(has_side_effects=True),
         name="exchange",
-    )(rot, local_weights, picked)
+    )(picked, key_grad, cosine, sine, key_quant, key_scales.T)
 
     margin = max(
         max(
@@ -447,15 +487,17 @@
         2 * quarter,
     ) if group_total > 1 else 2 * quarter
     pad = -(-(margin + slot_count) // 8) * 8
-    input_grad = pl.pallas_call(
+    return pl.pallas_call(
         functools.partial(assemble_kernel, owners_n, group_total, pad),
-        out_shape=jax.ShapeDtypeStruct((tokens_here, chunk), jnp.bfloat16),
-        in_specs=[smem, vmem],
-        out_specs=vmem,
+        out_shape=(
+            jax.ShapeDtypeStruct((slot_count, width), jnp.bfloat16),
+            jax.ShapeDtypeStruct((tokens_here, chunk), jnp.bfloat16),
+        ),
+        in_specs=[smem, vmem, vmem],
+        out_specs=(vmem,) * 2,
         scratch_shapes=[pltpu.VMEM((chunk + 2 * pad, tokens_here), jnp.float32)],
         name="assemble",
-    )(block_counts, pieces)
-    return (weight_grad.reshape(slot_count, width), input_grad)
+    )(block_counts, pieces, weight_grad)
 
 
 def rotary_backward(key_grad, positions):

time: 73.3 us -> 65.5 us (0.89)
  the two profiles are of different devices: /device:TPU:13 before, /device:TPU:0 now
where the time goes in v2:
time: 65.5 us; the launch traced here: 65.3 us
  Pallas kernels  63 us (96%)
  other arithmetic  1.62 us (2%)
    pallas_call x1, Pallas kernels, exchange_plan(): pl.pallas_call(functools.partial(exchange_kernel, owners_n, group_total),...  57 us
    pallas_call x1, Pallas kernels, exchange_plan(): pl.pallas_call(functools.partial(pick_kernel, owners_n, group_total, span...  3.43 us
    pallas_call x1, Pallas kernels, exchange_plan(): pl.pallas_call(functools.partial(assemble_kernel, owners_n, group_total,...  2.54 us

profile of v2, /device:TPU:0, one launch (start us, length us, event | category | flops | bytes accessed | tf_op | source)
XLA Modules:
  0.0 65.3 jit_solution(6791724078261897733)
XLA Ops:
  0.6 0.7 %convert_element_type.3 = f32[128]{0:T(128)S(1)} convert(s32[128]{0:T(128)} %param.8) | non-fusion elementwise | flops 128 | bytes 1024 | tf_op jit(solution)/shard_map/convert_element_type | solution.py:23
  1.3 1.0 %multiply_sine_fusion = (f32[128,64]{1,0:T(8,128)}, f32[128,64]{1,0:T(8,128)}) fusion(f32[64]{0:T(128)S(1)} %multiply_exponential_fusion, f32[128]{0:T(128)S(1)} %convert_element_type.3), kind=kLoop, calls=%fused_computation | loop fusion | flops 8192 | bytes 66304 | tf_op jit(solution)/shard_map/sin | solution.py:24
  2.3 3.4 %pick.1.picked_ref = bf16[8,272,128]{2,1,0:T(8,128)(2,1)} custom-call(s32[8]{0:T(128)} %counts_ref.3, bf16[128,8192]{1,0:T(8,128)(2,1)} %hidden_any.1), custom_call_target="tpu_custom_call" | custom-call | tf_op jit(solution)/shard_map/pick/pallas_call | solution.py:437
  5.7 57.0 %exchange.1 = (bf16[4,272,256]{2,1,0:T(8,128)(2,1)}, bf16[10,272,128]{2,1,0:T(8,128)(2,1)}) custom-call(bf16[8,272,128]{2,1,0:T(8,128)(2,1)} %pick.1.picked_ref, bf16[128,256]{1,0:T(8,128)(2,1)} %grad_ref.1, f32[128,64]{1,0:T(8,128)} %get-tuple-element.7.cos_ref, f32[128,64]{1,0:T(8,128)} %get-tuple-element.6.sin_ref, bf16[1088,256]{1,0:T(8,128)(2,1)} %quant_ref.1, ...), custom_call_target="tpu_custom_call" | custom-call | tf_op jit(solution)/shard_map/exchange/pallas_call | solution.py:452
  62.7 2.5 %assemble.1 = (bf16[1088,256]{1,0:T(8,128)(2,1)}, bf16[128,2048]{1,0:T(8,128)(2,1)}) custom-call(s32[8]{0:T(128)} %counts_ref.3, bf16[10,272,128]{2,1,0:T(8,128)(2,1)} %get-tuple-element.4.pieces_ref, bf16[4,272,256]{2,1,0:T(8,128)(2,1)} %get-tuple-element.5.grad_ref), custom_call_target="tpu_custom_call" | custom-call | tf_op jit(solution)/shard_map/assemble/pallas_call | solution.py:490
  (1 shorter events, 0.0 us)

commit v3 on v2

--- a/solution.py
+++ b/solution.py
@@ -139,6 +139,7 @@
     tokens, width = rot_ref.shape
     quarter = picked_ref.shape[1]
     half = width * group_total // 2
+    pieces = group_total // 2
     depth = owners_n // LINE
     z = here // LINE
     y = lax.rem(here, LINE)
@@ -185,13 +186,17 @@
             h_send.at[owner], h_recv.at[owner], (owner, part),
         )
 
-    def relay(owner, send, where):
-        view = rotated.at[rows_of(owner), pl.ds(pl.multiple_of(core * half, half), half)]
-        return remote(view, view, send.at[owner], net_recv.at[owner], (where, part))
-
-    def share(owner):
-        view = rotated.at[rows_of(owner), pl.ds(pl.multiple_of(core * half, half), half)]
-        return remote(view, view, pair_send.at[owner], pair_recv.at[owner], (here, partner))
+    def block_of(owner, piece):
+        first = core * half + piece * width
+        return rotated.at[rows_of(owner), pl.ds(pl.multiple_of(first, LANES), width)]
+
+    def relay(owner, send, where, piece):
+        view, at = block_of(owner, piece), owner * pieces + piece
+        return remote(view, view, send.at[at], net_recv.at[at], (where, part))
+
+    def share(owner, piece):
+        view, at = block_of(owner, piece), owner * pieces + piece
+        return remote(view, view, pair_send.at[at], pair_recv.at[at], (here, partner))
 
     own_rot = pltpu.make_async_copy(rot_ref, rotated.at[rows_of(here), cols_of(part)], own_sem.at[0])
     own_weights = pltpu.make_async_copy(
@@ -233,14 +238,14 @@
 
     below, above = here - LINE, here + LINE
 
-    def travel(owner, go_up, go_down, act):
+    def travel(owner, go_up, go_down, act, piece):
         @pl.when(go_up)
         def _():
-            act(relay(owner, up_send, above))
+            act(relay(owner, up_send, above, piece))
 
         @pl.when(go_down)
         def _():
-            act(relay(owner, down_send, below))
+            act(relay(owner, down_send, below, piece))
 
     def begin(copy):
         copy.start()
@@ -273,8 +278,9 @@
         def _():
             give(home - 1, last_piece, e_send.at[owner], 1)
 
-    travel(here, z < depth - 1, z > 0, begin)
-    relay(here, side_send, beside).start()
+    for piece in range(pieces):
+        travel(here, z < depth - 1, z > 0, begin, piece)
+        relay(here, side_send, beside, piece).start()
     hide_at(1, False)
     hide_at(-1, False)
 
@@ -283,11 +289,6 @@
             weights[...], rotated[rows_of(owner), :], (((1,), (1,)), ((), ())),
             preferred_element_type=jnp.float32,
         ).astype(jnp.bfloat16)
-
-    own_weights.wait()
-    for step in range(1, group_total):
-        weigh(step).wait_recv()
-    produce(here)
 
     def stage_items(away):
         items = []
@@ -298,7 +299,6 @@
                 items.append((z + sign * (away - 1), 1 - y))
         return items
 
-    send_piece(here, begin, begin)
     for away in range(1, depth + 2):
         for sign in (-1, 1):
             if away < depth:
@@ -307,13 +307,14 @@
 
                 @pl.when((level >= 0) & (level < depth))
                 def _():
-                    relay(owner, up_send, here).wait_recv()
-                    if sign < 0:
-                        travel(owner, z < depth - 1, z < 0, begin)
-                    else:
-                        travel(owner, z < 0, z > 0, begin)
-                    relay(owner, side_send, beside).start()
-                    share(owner).start()
+                    for piece in range(pieces):
+                        relay(owner, up_send, here, piece).wait_recv()
+                        if sign < 0:
+                            travel(owner, z < depth - 1, z < 0, begin, piece)
+                        else:
+                            travel(owner, z < 0, z > 0, begin, piece)
+                        relay(owner, side_send, beside, piece).start()
+                        share(owner, piece).start()
 
             if away <= depth and (away > 1 or sign < 0):
                 level_near = z + sign * (away - 1)
@@ -321,8 +322,9 @@
 
                 @pl.when((level_near >= 0) & (level_near < depth))
                 def _():
-                    relay(other, up_send, here).wait_recv()
-                    share(other).start()
+                    for piece in range(pieces):
+                        relay(other, up_send, here, piece).wait_recv()
+                        share(other, piece).start()
 
         if away < depth:
             hide_at(away, True)
@@ -330,12 +332,19 @@
         if away + 1 < depth:
             hide_at(away + 1, False)
             hide_at(-away - 1, False)
+        if away == 2:
+            own_weights.wait()
+            for step in range(1, group_total):
+                weigh(step).wait_recv()
+            produce(here)
+            send_piece(here, begin, begin)
         ready = stage_items(away - 1)
         for level, row in ready:
 
             @pl.when((level >= 0) & (level < depth))
             def _():
-                share(level * LINE + row).wait_recv()
+                for piece in range(pieces):
+                    share(level * LINE + row, piece).wait_recv()
                 produce(level * LINE + row)
 
         for level, row in ready:
@@ -398,8 +407,9 @@
         weigh(step).wait_send()
     for step in range(1, owners_n):
         hide(lax.rem(here + step, owners_n)).wait_send()
-    travel(here, z < depth - 1, z > 0, finish)
-    relay(here, side_send, beside).wait_send()
+    for piece in range(pieces):
+        travel(here, z < depth - 1, z > 0, finish, piece)
+        relay(here, side_send, beside, piece).wait_send()
     for away in range(1, depth):
         for sign in (-1, 1):
             level = z + sign * away
@@ -407,14 +417,16 @@
 
             @pl.when((level >= 0) & (level < depth))
             def _():
-                if sign < 0:
-                    travel(owner, z < depth - 1, z < 0, finish)
-                else:
-                    travel(owner, z < 0, z > 0, finish)
-                relay(owner, side_send, beside).wait_send()
+                for piece in range(pieces):
+                    if sign < 0:
+                        travel(owner, z < depth - 1, z < 0, finish, piece)
+                    else:
+                        travel(owner, z < 0, z > 0, finish, piece)
+                    relay(owner, side_send, beside, piece).wait_send()
 
     def drain(step, carry):
-        share(lax.rem(here + step, owners_n)).wait_send()
+        for piece in range(pieces):
+            share(lax.rem(here + step, owners_n), piece).wait_send()
         return carry
 
     lax.fori_loop(1, owners_n, drain, 0)
@@ -447,6 +459,7 @@
         name="pick",
     )(block_counts, hidden_in)
 
+    relays_n = owners_n * group_total // 2
     pieces_n = 2 + per_chunk * group_total
     dma = pltpu.SemaphoreType.DMA
     weight_grad, pieces = pl.pallas_call(
@@ -469,8 +482,8 @@
             dma((group_total - 1,)), dma((group_total - 1,)),
             dma((group_total - 1,)), dma((group_total - 1,)),
             dma((owners_n,)), dma((owners_n,)),
-            dma((owners_n,)), dma((owners_n,)), dma((owners_n,)), dma((owners_n,)),
-            dma((owners_n,)), dma((owners_n,)),
+            dma((relays_n,)), dma((relays_n,)), dma((relays_n,)), dma((relays_n,)),
+            dma((relays_n,)), dma((relays_n,)),
             dma((owners_n,)), dma((owners_n,)), dma((pieces_n,)),
             dma((group_total - 1,)), dma((group_total - 1,)),
             dma((2,)),

time: 65.5 us -> 63.4 us (0.968)
  the two profiles are of different devices: /device:TPU:0 before, /device:TPU:5 now
where the time goes in v3:
time: 63.4 us; the launch traced here: 63.2 us
  Pallas kernels  60.9 us (96%)
  other arithmetic  1.62 us (3%)
  between operations  0.65 us (1%)
    pallas_call x1, Pallas kernels, exchange_plan(): pl.pallas_call(functools.partial(exchange_kernel, owners_n, group_total),...  54.9 us
    pallas_call x1, Pallas kernels, exchange_plan(): pl.pallas_call(functools.partial(pick_kernel, owners_n, group_total, span...  3.42 us
    pallas_call x1, Pallas kernels, exchange_plan(): pl.pallas_call(functools.partial(assemble_kernel, owners_n, group_total,...  2.54 us

profile of v3, /device:TPU:5, one launch (start us, length us, event | category | flops | bytes accessed | tf_op | source)
XLA Modules:
  0.0 63.2 jit_solution(11418824652046268486)
XLA Ops:
  0.6 0.7 %convert_element_type.3 = f32[128]{0:T(128)S(1)} convert(s32[128]{0:T(128)} %param.8) | non-fusion elementwise | flops 128 | bytes 1024 | tf_op jit(solution)/shard_map/convert_element_type | solution.py:23
  1.3 1.0 %multiply_sine_fusion = (f32[128,64]{1,0:T(8,128)}, f32[128,64]{1,0:T(8,128)}) fusion(f32[64]{0:T(128)S(1)} %multiply_exponential_fusion, f32[128]{0:T(128)S(1)} %convert_element_type.3), kind=kLoop, calls=%fused_computation | loop fusion | flops 8192 | bytes 66304 | tf_op jit(solution)/shard_map/sin | solution.py:24
  2.3 3.4 %pick.1.picked_ref = bf16[8,272,128]{2,1,0:T(8,128)(2,1)} custom-call(s32[8]{0:T(128)} %counts_ref.3, bf16[128,8192]{1,0:T(8,128)(2,1)} %hidden_any.1), custom_call_target="tpu_custom_call" | custom-call | tf_op jit(solution)/shard_map/pick/pallas_call | solution.py:449
  5.7 54.9 %exchange.1 = (bf16[4,272,256]{2,1,0:T(8,128)(2,1)}, bf16[10,272,128]{2,1,0:T(8,128)(2,1)}) custom-call(bf16[8,272,128]{2,1,0:T(8,128)(2,1)} %pick.1.picked_ref, bf16[128,256]{1,0:T(8,128)(2,1)} %grad_ref.1, f32[128,64]{1,0:T(8,128)} %get-tuple-element.7.cos_ref, f32[128,64]{1,0:T(8,128)} %get-tuple-element.6.sin_ref, bf16[1088,256]{1,0:T(8,128)(2,1)} %quant_ref.1, ...), custom_call_target="tpu_custom_call" | custom-call | tf_op jit(solution)/shard_map/exchange/pallas_call | solution.py:465
  60.6 2.5 %assemble.1 = (bf16[1088,256]{1,0:T(8,128)(2,1)}, bf16[128,2048]{1,0:T(8,128)(2,1)}) custom-call(s32[8]{0:T(128)} %counts_ref.3, bf16[10,272,128]{2,1,0:T(8,128)(2,1)} %get-tuple-element.4.pieces_ref, bf16[4,272,256]{2,1,0:T(8,128)(2,1)} %get-tuple-element.5.grad_ref), custom_call_target="tpu_custom_call" | custom-call | tf_op jit(solution)/shard_map/assemble/pallas_call | solution.py:503
  (1 shorter events, 0.0 us)
